TPU v7x, 32 devices: a whole 2x2x4 slice. The times are simulated.
32 devices in a mesh: dp: 8 (over y, x, core), tensor: 4 (over z).
Axes of the slice: x: 2, y: 2, z: 4, core: 2. Of those that a mesh axis runs over, the one named last changes fastest.
Arguments:
- tokens: bfloat16 [512, 8192], P('dp'), may hold values from -6 to 6
- gate_weight: bfloat16 [8192, 14848], P('dp', 'tensor'), may hold values from -0.09375 to 0.09375
- up_weight: bfloat16 [8192, 14848], P('dp', 'tensor'), may hold values from -0.09375 to 0.09375
- down_weight: bfloat16 [14848, 8192], P('tensor', 'dp'), may hold values from -6 to 6
- channel_group: int32 [14848], P('tensor'), may hold values from 0 to 115, as said below
- owners: int32 [116], replicated, may hold values from 0 to 3
Outputs:
- group_scores: float32 [4, 116], P('tensor')
Inputs may be any that keep to these rules, and one draw needn't show every extreme that they name: `channel_group`: every group 0 to 115 has exactly 128 channels.
All inputs are finite; a program needn't handle non-finite values.
Results may differ from a plain program's by a relative error of at most 0.0044.
Values may be sent and summed in bfloat16 or wider, within the bound.
A program may use at most 128 MiB of HBM per device.

v0:
```python
import functools

import jax
import jax.numpy as jnp
from jax import lax
from jax.experimental import pallas as pl
from jax.experimental.pallas import tpu as pltpu
from jax.sharding import PartitionSpec as P

GROUP = 128
LANES = 128
LAG_CORE = 3
LAG_FIRST = 8
LAG_SECOND = 13
MESH = pl.DeviceIdType.MESH


def group_sum(channel_score, groups, count):
    onehot = (groups[:, None] == jnp.arange(count, dtype=jnp.int32)[None, :]).astype(jnp.float32)
    return jnp.dot(channel_score, onehot, precision=lax.Precision.HIGHEST) / GROUP


def plain_shards(tokens, gate_weight, up_weight, down_weight, channel_group, owners):
    total_tokens = tokens.shape[0] * lax.axis_size("dp")
    width = gate_weight.shape[1]
    group_count = owners.shape[0]
    magnitude = jnp.sum(jnp.abs(down_weight.astype(jnp.float32)), axis=1) / tokens.shape[1]
    columns = lax.all_to_all(tokens, "dp", split_axis=1, concat_axis=0, tiled=True)
    mixed = lax.psum_scatter(
        jnp.concatenate(
            (
                jnp.dot(columns, gate_weight, preferred_element_type=jnp.float32),
                jnp.dot(columns, up_weight, preferred_element_type=jnp.float32),
            ),
            axis=1,
        ).astype(jnp.bfloat16),
        "dp",
        scatter_dimension=0,
        tiled=True,
    ).astype(jnp.float32)
    hidden = jax.nn.silu(mixed[:, :width]) * mixed[:, width:]
    energy = jnp.sum(hidden * hidden, axis=0) / total_tokens
    energy, magnitude = lax.psum((energy, magnitude), "dp")
    partial_value = group_sum(jnp.sqrt(energy) * magnitude, channel_group, group_count)
    totals = lax.psum(partial_value, "tensor")
    rank = lax.axis_index("tensor")
    row = jnp.where(owners == rank, totals, jnp.float32(0.0))
    return row[None, :]


def kernel(
    n_tensor,
    tok_ref,
    gate_ref,
    up_ref,
    down_ref,
    group_ref,
    owner_ref,
    out_ref,
    tok_buf,
    x_buf,
    w_buf,
    d_buf,
    part,
    got_core,
    got_first,
    got_second,
    energy,
    magnitude,
    score,
    totals,
    x_send,
    x_recv,
    local_sem,
    g_sem,
    u_sem,
    d_sem,
    core_send,
    core_recv,
    first_send,
    first_recv,
    second_send,
    second_recv,
    m_send,
    m_recv,
    early_send,
    early_recv,
    e_send,
    e_recv,
    t_send,
    t_recv,
):
    n_dp = 8
    chunks = w_buf.shape[0]
    block = tok_ref.shape[0]
    depth = x_buf.shape[1]
    me = lax.axis_index("dp")
    z = lax.axis_index("tensor")
    c, x, y = me % 2, (me // 2) % 2, me // 4
    x_peer = me + 2 * (1 - 2 * x)
    y_peer = me + 4 * (1 - 2 * y)
    core_peer = me + (1 - 2 * c)
    first_peer = (1 - c) * x_peer + c * y_peer
    second_peer = (1 - c) * y_peer + c * x_peer

    def peer_of(k):
        bc, bx, by = k % 2, (k // 2) % 2, k // 4
        return me + bc * (1 - 2 * c) + 2 * bx * (1 - 2 * x) + 4 * by * (1 - 2 * y)

    def remote(src, dst, send, recv, peer):
        return pltpu.make_async_remote_copy(
            src_ref=src, dst_ref=dst, send_sem=send, recv_sem=recv, device_id=(peer, z), device_id_type=MESH
        )

    def gate_copy(i):
        cols = pl.ds(pl.multiple_of(i * LANES, LANES), LANES)
        return pltpu.make_async_copy(gate_ref.at[:, cols], w_buf.at[i, :, pl.ds(0, LANES)], g_sem.at[i])

    def up_copy(i):
        cols = pl.ds(pl.multiple_of(i * LANES, LANES), LANES)
        return pltpu.make_async_copy(up_ref.at[:, cols], w_buf.at[i, :, pl.ds(LANES, LANES)], u_sem.at[i])

    def down_copy(i):
        rows = pl.ds(pl.multiple_of(i * LANES, LANES), LANES)
        return pltpu.make_async_copy(down_ref.at[rows, :], d_buf.at[i], d_sem.at[i])

    load_tokens = pltpu.make_async_copy(tok_ref, tok_buf, local_sem)
    load_tokens.start()
    barrier = pltpu.get_barrier_semaphore()
    for k in range(1, n_dp):
        pl.semaphore_signal(barrier, inc=1, device_id=(peer_of(k), z), device_id_type=MESH)
    for k in range(1, n_tensor):
        pl.semaphore_signal(barrier, inc=1, device_id=(me, (z + k) % n_tensor), device_id_type=MESH)

    own_cols = pl.ds(pl.multiple_of(me * depth, depth), depth)

    @pl.loop(0, chunks)
    def _(i):
        down_copy(i).start()

    load_tokens.wait()
    pl.semaphore_wait(barrier, n_dp - 1 + n_tensor - 1)

    token_copies = []
    for k in (6, 7, 2, 3, 4, 5, 1):
        bc, bx, by = k % 2, (k // 2) % 2, k // 4
        slot = bc * 4 + (1 - c) * (2 * bx + by) + c * (2 * by + bx)
        peer = peer_of(k)
        cols = pl.ds(pl.multiple_of(peer * depth, depth), depth)
        rows = pl.ds(pl.multiple_of(slot * block, block), block)
        copy = remote(tok_buf.at[:, cols], x_buf.at[rows, :], x_send.at[k - 1], x_recv.at[k - 1], peer)
        copy.start()
        token_copies.append(copy)

    @pl.loop(0, chunks)
    def _(i):
        gate_copy(i).start()
        up_copy(i).start()

    ones = jnp.ones((8, d_buf.shape[2]), jnp.bfloat16)

    @pl.loop(0, chunks)
    def _(i):
        down_copy(i).wait()
        sums = lax.dot_general(
            ones, jnp.abs(d_buf[i]), (((1,), (1,)), ((), ())), preferred_element_type=jnp.float32
        )
        magnitude[me, pl.ds(i, 1), :] = sums[0:1, :]

    x_buf[:block, :] = tok_buf[:, own_cols]
    for copy in token_copies:
        copy.wait()

    m_copies = []
    for k in range(1, n_dp):
        copy = remote(magnitude.at[me], magnitude.at[me], m_send.at[k - 1], m_recv.at[k - 1], peer_of(k))
        copy.start()
        m_copies.append(copy)

    early = (chunks - 1) // 8 * 8

    def early_copy(k):
        rows = energy.at[me, pl.ds(0, early), :]
        return remote(rows, rows, early_send.at[k - 1], early_recv.at[k - 1], peer_of(k))

    def late_copy(k):
        rows = energy.at[me, pl.ds(early, chunks - early), :]
        return remote(rows, rows, e_send.at[k - 1], e_recv.at[k - 1], peer_of(k))

    half, quarter, eighth = 4 * block, 2 * block, block

    def core_copy(i):
        return remote(
            part.at[i, pl.ds(half, half), :], got_core.at[i], core_send.at[i], core_recv.at[i], core_peer
        )

    def first_copy(i):
        return remote(
            part.at[i, pl.ds(quarter, quarter), :], got_first.at[i], first_send.at[i], first_recv.at[i], first_peer
        )

    def second_copy(i):
        return remote(
            part.at[i, pl.ds(eighth, eighth), :], got_second.at[i], second_send.at[i], second_recv.at[i], second_peer
        )

    def add(a, b):
        return (a.astype(jnp.float32) + b.astype(jnp.float32)).astype(jnp.bfloat16)

    def step(it, on):
        after_core, after_first, after_second = it - LAG_CORE, it - LAG_FIRST, it - LAG_SECOND

        @pl.when((after_core >= 0) & (after_core < chunks))
        def _():
            core_copy(after_core).wait_recv()
            part[after_core, :half, :] = add(part[after_core, :half, :], got_core[after_core])

        @pl.when((after_first >= 0) & (after_first < chunks))
        def _():
            first_copy(after_first).wait_recv()
            part[after_first, :quarter, :] = add(part[after_first, :quarter, :], got_first[after_first])

        @pl.when(it < chunks)
        def _():
            gate_copy(it).wait()
            up_copy(it).wait()
            part[it, half:, :] = jnp.dot(
                x_buf[half:, :], w_buf[it], preferred_element_type=jnp.float32
            ).astype(jnp.bfloat16)
            part[it, :half, :] = jnp.dot(
                x_buf[:half, :], w_buf[it], preferred_element_type=jnp.float32
            ).astype(jnp.bfloat16)

        @pl.when((after_first >= 0) & (after_first < chunks))
        def _():
            second_copy(after_first).start()

        @pl.when((after_core >= 0) & (after_core < chunks))
        def _():
            first_copy(after_core).start()

        @pl.when(it < chunks)
        def _():
            core_copy(it).start()

        @pl.when(after_second == early)
        def _():
            for k in range(1, n_dp):
                early_copy(k).start()

        @pl.when(after_second >= 0)
        def _():
            second_copy(after_second).wait_recv()
            mixed = part[after_second, :eighth, :].astype(jnp.float32) + got_second[after_second].astype(jnp.float32)
            gate, up = mixed[:, :LANES], mixed[:, LANES:]
            hidden = gate / (1.0 + jnp.exp(-gate)) * up
            energy[me, pl.ds(after_second, 1), :] = jnp.sum(hidden * hidden, axis=0, keepdims=True)

        return on

    lax.fori_loop(0, chunks + LAG_SECOND, step, 0)

    for k in range(1, n_dp):
        late_copy(k).start()
    for copy in m_copies:
        copy.wait()
    mag = magnitude[0]
    for r in range(1, n_dp):
        mag = mag + magnitude[r]
    mag = mag / tok_ref.shape[1]
    for k in range(1, n_dp):
        early_copy(k).wait()
        late_copy(k).wait_recv()
    total = energy[0]
    for r in range(1, n_dp):
        total = total + energy[r]
    score[...] = jnp.sqrt(total / (block * n_dp)) * mag

    lines = lax.broadcasted_iota(jnp.int32, (score_groups(owner_ref), LANES), 0)

    def gather(i, acc):
        hit = lines == group_ref[pl.ds(i, 1), :]
        return acc + jnp.where(hit, score[pl.ds(i, 1), :], 0.0)

    acc = lax.fori_loop(0, chunks, gather, jnp.zeros(lines.shape, jnp.float32))
    mine = jnp.sum(acc.T, axis=0, keepdims=True)
    totals[z] = jnp.broadcast_to(mine, totals.shape[1:])
    t_copies = []
    for k in range(1, n_tensor):
        copy = pltpu.make_async_remote_copy(
            src_ref=totals.at[z],
            dst_ref=totals.at[z],
            send_sem=t_send.at[k - 1],
            recv_sem=t_recv.at[k - 1],
            device_id=(me, (z + k) % n_tensor),
            device_id_type=MESH,
        )
        copy.start()
        t_copies.append(copy)

    for k in range(1, n_dp):
        late_copy(k).wait_send()

    @pl.loop(0, chunks)
    def _(i):
        core_copy(i).wait_send()
        first_copy(i).wait_send()
        second_copy(i).wait_send()

    for copy in t_copies:
        copy.wait()
    row = totals[0]
    for r in range(1, n_tensor):
        row = row + totals[r]
    row = row[0:1, : out_ref.shape[1]] / GROUP
    out_ref[...] = jnp.where(owner_ref[...] == z, row, 0.0)


def score_groups(owner_ref):
    return -(-owner_ref.shape[1] // LANES) * LANES


def fused_shards(n_dp, n_tensor, tokens, gate_weight, up_weight, down_weight, channel_group, owners):
    block = tokens.shape[0]
    depth, width = gate_weight.shape
    chunks = width // LANES
    count = owners.shape[0]
    span = down_weight.shape[1]
    rows = block * n_dp
    vmem = pl.BlockSpec(memory_space=pltpu.VMEM)
    hbm = pl.BlockSpec(memory_space=pl.ANY)
    padded = -(-count // LANES) * LANES
    dma = pltpu.SemaphoreType.DMA
    return pl.pallas_call(
        functools.partial(kernel, n_tensor),
        out_shape=jax.ShapeDtypeStruct((1, count), jnp.float32),
        in_specs=[hbm, hbm, hbm, hbm, vmem, vmem],
        out_specs=vmem,
        scratch_shapes=[
            pltpu.VMEM(tokens.shape, jnp.bfloat16),
            pltpu.VMEM((rows, depth), jnp.bfloat16),
            pltpu.VMEM((chunks, depth, 2 * LANES), jnp.bfloat16),
            pltpu.VMEM((chunks, LANES, span), jnp.bfloat16),
            pltpu.VMEM((chunks, rows, 2 * LANES), jnp.bfloat16),
            pltpu.VMEM((chunks, rows // 2, 2 * LANES), jnp.bfloat16),
            pltpu.VMEM((chunks, rows // 4, 2 * LANES), jnp.bfloat16),
            pltpu.VMEM((chunks, rows // 8, 2 * LANES), jnp.bfloat16),
            pltpu.VMEM((n_dp, chunks, LANES), jnp.float32),
            pltpu.VMEM((n_dp, chunks, LANES), jnp.float32),
            pltpu.VMEM((chunks, LANES), jnp.float32),
            pltpu.VMEM((n_tensor, 8, padded), jnp.float32),
            dma((n_dp - 1,)),
            dma((n_dp - 1,)),
            dma,
            dma((chunks,)),
            dma((chunks,)),
            dma((chunks,)),
            dma((chunks,)),
            dma((chunks,)),
            dma((chunks,)),
            dma((chunks,)),
            dma((chunks,)),
            dma((chunks,)),
            dma((n_dp - 1,)),
            dma((n_dp - 1,)),
            dma((n_dp - 1,)),
            dma((n_dp - 1,)),
            dma((n_dp - 1,)),
            dma((n_dp - 1,)),
            dma((max(n_tensor - 1, 1),)),
            dma((max(n_tensor - 1, 1),)),
        ],
        compiler_params=pltpu.CompilerParams(
            collective_id=0, has_side_effects=True, vmem_limit_bytes=56 * 1024 * 1024
        ),
    )(tokens, gate_weight, up_weight, down_weight, channel_group.reshape(chunks, LANES), owners.reshape(1, count))


def solution(mesh):
    n_dp, n_tensor = mesh.shape["dp"], mesh.shape["tensor"]

    def shards(tokens, gate_weight, *rest):
        if n_dp == 8 and gate_weight.shape[1] % LANES == 0:
            return fused_shards(n_dp, n_tensor, tokens, gate_weight, *rest)
        return plain_shards(tokens, gate_weight, *rest)

    return jax.shard_map(
        shards,
        mesh=mesh,
        in_specs=(
            P("dp", None),
            P("dp", "tensor"),
            P("dp", "tensor"),
            P("tensor", "dp"),
            P("tensor"),
            P(),
        ),
        out_specs=P("tensor", None),
        check_vma=False,
    )
```

profile of v0, /device:TPU:0, one launch (start us, length us, event | category | flops | bytes accessed | tf_op | source)
XLA Modules:
  0.0 69.2 jit_solution(10408567916213345325)
XLA Ops:
  0.0 68.0 %shard_map.64 = f32[1,116]{1,0:T(1,128)} custom-call(bf16[64,8192]{1,0:T(8,128)(2,1)} %tok_ref.1, bf16[1024,3712]{1,0:T(8,128)(2,1)} %gate_ref.1, bf16[1024,3712]{1,0:T(8,128)(2,1)} %up_ref.1, bf16[3712,1024]{1,0:T(8,128)(2,1)} %down_ref.1, s32[29,128]{1,0:T(8,128)} %bitcast.2, s32[1,116]{1,0:T(1,128)} %bitcast.3), custom_call_target="tpu_custom_call" | custom-call | tf_op jit(solution)/shard_map/pallas_call | solution.py:334
  68.0 1.2 %copy.8 = f32[1,116]{1,0:T(1,128)} copy(f32[1,116]{1,0:T(1,128)} %shard_map.64) | data formatting | bytes 928
where the time goes:
time: 69.4 us; the launch traced here: 69.2 us
  Pallas kernels  68 us (98%)
  local copies, waits for them, and re-layouts  1.19 us (2%)
    pallas_call x1, Pallas kernels, fused_shards(): pl.pallas_call(functools.partial(kernel, n_tensor), out_shape=jax.ShapeDt...  68 us

commit v1 on v0

v1 whole, which is shorter than its diff:
```python
import functools

import jax
import jax.numpy as jnp
from jax import lax
from jax.experimental import pallas as pl
from jax.experimental.pallas import tpu as pltpu
from jax.sharding import PartitionSpec as P

GROUP = 128
LANES = 128
ROLES = 4
LAG_CORE = 2
LAG_FIRST = 7
LAG_SECOND = 3
MESH = pl.DeviceIdType.MESH


def group_sum(channel_score, groups, count):
    onehot = (groups[:, None] == jnp.arange(count, dtype=jnp.int32)[None, :]).astype(jnp.float32)
    return jnp.dot(channel_score, onehot, precision=lax.Precision.HIGHEST) / GROUP


def plain_shards(tokens, gate_weight, up_weight, down_weight, channel_group, owners):
    total_tokens = tokens.shape[0] * lax.axis_size("dp")
    width = gate_weight.shape[1]
    group_count = owners.shape[0]
    magnitude = jnp.sum(jnp.abs(down_weight.astype(jnp.float32)), axis=1) / tokens.shape[1]
    columns = lax.all_to_all(tokens, "dp", split_axis=1, concat_axis=0, tiled=True)
    mixed = lax.psum_scatter(
        jnp.concatenate(
            (
                jnp.dot(columns, gate_weight, preferred_element_type=jnp.float32),
                jnp.dot(columns, up_weight, preferred_element_type=jnp.float32),
            ),
            axis=1,
        ).astype(jnp.bfloat16),
        "dp",
        scatter_dimension=0,
        tiled=True,
    ).astype(jnp.float32)
    hidden = jax.nn.silu(mixed[:, :width]) * mixed[:, width:]
    energy = jnp.sum(hidden * hidden, axis=0) / total_tokens
    energy, magnitude = lax.psum((energy, magnitude), "dp")
    partial_value = group_sum(jnp.sqrt(energy) * magnitude, channel_group, group_count)
    totals = lax.psum(partial_value, "tensor")
    rank = lax.axis_index("tensor")
    row = jnp.where(owners == rank, totals, jnp.float32(0.0))
    return row[None, :]


def kernel(
    n_tensor,
    tok_ref,
    gate_ref,
    up_ref,
    down_ref,
    group_ref,
    owner_ref,
    out_ref,
    tok_buf,
    x_buf,
    w_buf,
    d_buf,
    group_buf,
    owner_buf,
    give,
    keep,
    got_core,
    got_first,
    got_second,
    give_x,
    keep_x,
    got_core_x,
    got_first_x,
    got_second_x,
    energy,
    shared,
    mag_out,
    magnitude,
    score,
    totals,
    local_sem,
    g_sem,
    u_sem,
    d_sem,
    x_send,
    x_recv,
    core_send,
    core_recv,
    first_send,
    first_recv,
    second_send,
    second_recv,
    core_x_send,
    core_x_recv,
    first_x_send,
    first_x_recv,
    second_x_send,
    second_x_recv,
    m_send,
    m_recv,
    s_send,
    s_recv,
    e_send,
    e_recv,
    t_send,
    t_recv,
    seen,
):
    n_dp = 8
    chunks = w_buf.shape[0]
    quads, extra = chunks // ROLES, chunks % ROLES
    items = 4 * quads
    block = tok_ref.shape[0]
    depth = x_buf.shape[2]
    me = lax.axis_index("dp")
    z = lax.axis_index("tensor")
    c, x, y = me % 2, (me // 2) % 2, me // 4
    chip = me // 2

    def chip_at(f, s):
        fx, fy = f * (1 - c) + s * c, f * c + s * (1 - c)
        return 2 * (y + fy * (1 - 2 * y)) + x + fx * (1 - 2 * x)

    def device_at(f, s, same):
        return 2 * chip_at(f, s) + (c if same else 1 - c)

    core_peer = device_at(0, 0, False)
    first_peer = device_at(1, 0, True)
    second_peer = device_at(0, 1, True)
    others = [(r % 2, r // 2, same) for r in range(4) for same in (False, True) if (r, same) != (0, True)]

    def remote(src, dst, send, recv, peer, plane=z):
        return pltpu.make_async_remote_copy(
            src_ref=src, dst_ref=dst, send_sem=send, recv_sem=recv, device_id=(peer, plane), device_id_type=MESH
        )

    barrier = pltpu.get_barrier_semaphore()
    near = [hop for hop in others if hop[0] + hop[1] < 2]
    for hop in near:
        pl.semaphore_signal(barrier, inc=1, device_id=(device_at(*hop), z), device_id_type=MESH)

    def signal_planes(sem):
        @pl.when(z > 0)
        def _():
            pl.semaphore_signal(sem, inc=1, device_id=(me, z - 1), device_id_type=MESH)

        @pl.when(z < n_tensor - 1)
        def _():
            pl.semaphore_signal(sem, inc=1, device_id=(me, z + 1), device_id_type=MESH)

    planes = jnp.where(z > 0, 1, 0) + jnp.where(z < n_tensor - 1, 1, 0)
    signal_planes(barrier)

    load_tokens = pltpu.make_async_copy(tok_ref, tok_buf, local_sem.at[0])
    load_groups = pltpu.make_async_copy(group_ref, group_buf, local_sem.at[1])
    load_owners = pltpu.make_async_copy(owner_ref, owner_buf, local_sem.at[2])
    load_tokens.start()

    def gate_copy(i):
        cols = pl.ds(pl.multiple_of(i * LANES, LANES), LANES)
        return pltpu.make_async_copy(gate_ref.at[:, cols], w_buf.at[i, :, pl.ds(0, LANES)], g_sem.at[i])

    def up_copy(i):
        cols = pl.ds(pl.multiple_of(i * LANES, LANES), LANES)
        return pltpu.make_async_copy(up_ref.at[:, cols], w_buf.at[i, :, pl.ds(LANES, LANES)], u_sem.at[i])

    def down_copy(i):
        rows = pl.ds(pl.multiple_of(i * LANES, LANES), LANES)
        return pltpu.make_async_copy(down_ref.at[rows, :], d_buf.at[i], d_sem.at[i])

    for i in list(range(ROLES)) + list(range(chunks - extra, chunks)):
        gate_copy(i).start()
        up_copy(i).start()

    @pl.loop(ROLES, chunks - extra)
    def _(i):
        gate_copy(i).start()
        up_copy(i).start()

    def token_copy(r, same):
        peer = device_at(r % 2, r // 2, same)
        cols = pl.ds(pl.multiple_of(peer * depth, depth), depth)
        slot = 2 * r + (1 if same else 0)
        rows = pl.ds(block if same else 0, block)
        return remote(tok_buf.at[:, cols], x_buf.at[r, rows, :], x_send.at[slot], x_recv.at[slot], peer)

    load_tokens.wait()
    pl.semaphore_wait(barrier, len(near) + planes)
    token_copy(0, False).start()
    for same in (True, False):
        token_copy(1, same).start()
    load_groups.start()
    load_owners.start()

    @pl.loop(0, chunks)
    def _(i):
        down_copy(i).start()

    own_cols = pl.ds(pl.multiple_of(me * depth, depth), depth)
    x_buf[0, block:, :] = tok_buf[:, own_cols]
    mag_out[...] = jnp.zeros_like(mag_out)
    energy[...] = jnp.zeros_like(energy)
    shared[...] = jnp.zeros_like(shared)
    ones = jnp.ones((8, d_buf.shape[2]), jnp.bfloat16)

    def other_row(j, step):
        r = j // quads
        return j + quads * (step - 2 * step * ((r // step) % 2))

    def core_copy(j):
        return remote(give.at[j], got_core.at[j], core_send.at[j], core_recv.at[j], core_peer)

    def first_copy(j, to):
        return remote(keep.at[j, pl.ds(2, 2)], got_first.at[to], first_send.at[j], first_recv.at[to], first_peer)

    def second_copy(j, to):
        return remote(keep.at[j, 1], got_second.at[to], second_send.at[j], second_recv.at[to], second_peer)

    def core_x_copy(r, e):
        j = r * extra + e
        return remote(give_x.at[j], got_core_x.at[j], core_x_send.at[j], core_x_recv.at[j], core_peer)

    def first_x_copy(half, e):
        j = half * extra + e
        source = (2 * half + 1) * extra + e
        return remote(keep_x.at[source], got_first_x.at[j], first_x_send.at[j], first_x_recv.at[j], first_peer)

    def second_x_copy(e):
        return remote(
            keep_x.at[2 * extra + e], got_second_x.at[e], second_x_send.at[e], second_x_recv.at[e], second_peer
        )

    def share_copy(n):
        return remote(shared.at[me], shared.at[me], s_send.at[n], s_recv.at[n], device_at(*others[n]))

    def magnitude_copy(n):
        f, s, same = others[n]
        return remote(mag_out.at[chip_at(f, s)], magnitude.at[me], m_send.at[n], m_recv.at[n], device_at(f, s, same))

    def total(*refs):
        value = refs[0].astype(jnp.float32)
        for ref in refs[1:]:
            value = value + ref.astype(jnp.float32)
        return value

    def squares(mixed):
        gate, up = mixed[:, :LANES], mixed[:, LANES:]
        hidden = gate / (1.0 + jnp.exp(-gate)) * up
        return jnp.sum(hidden * hidden, axis=0, keepdims=True)

    swap = (0, 2, 1, 3)
    magnitude_start = quads + 1
    magnitude_end = magnitude_start + -(-chunks // 2)
    last_fold = 3 * quads + LAG_FIRST
    steps = last_fold + LAG_SECOND + quads
    rounds = [(quads + 2) + 4 * n for n in range(n_tensor - 1)]

    token_copy(0, False).wait_recv()

    def step(it, on):
        after_core = it - LAG_CORE
        after_first = it - LAG_FIRST
        final = it - last_fold - LAG_SECOND
        r = it // quads
        core_row = after_core // quads
        for k in range(1, 4):

            @pl.when(it == k * quads)
            def _():
                token_copy(k, False).wait_recv()
                token_copy(k, True).wait_recv()

        @pl.when(it == 2)
        def _():
            for same in (True, False):
                token_copy(2, same).start()

        @pl.when(it == quads)
        def _():
            for same in (True, False):
                token_copy(3, same).start()

        for n, at in enumerate(rounds):

            @pl.when(it == at)
            def _():
                if n > 0:
                    pl.semaphore_wait(seen.at[n - 1], planes)
                signal_planes(seen.at[n])

        @pl.when((after_core >= 0) & (after_core < items))
        def _():
            core_copy(after_core).wait_recv()
            keep[after_core, 2:] = total(keep[after_core, 2:], got_core[after_core, 2:]).astype(jnp.bfloat16)

        if extra:

            @pl.when((after_core >= 0) & (after_core < items) & (after_core % quads == 0))
            def _():
                for e in range(extra):
                    core_x_copy(core_row, e).wait_recv()
                    j = core_row * extra + e
                    keep_x[j] = jnp.where(
                        core_row % 2 == 1, total(keep_x[j], got_core_x[j]), keep_x[j].astype(jnp.float32)
                    ).astype(jnp.bfloat16)

        @pl.when(it < items)
        def _():
            u = it % quads

            @pl.when(r == 0)
            def _():
                for k in range(ROLES):
                    gate_copy(ROLES * u + k).wait()
                    up_copy(ROLES * u + k).wait()

            for role in (2, 3, 1, 0):
                product = jnp.dot(
                    x_buf[r], w_buf[ROLES * u + chip_at(role // 2, role % 2)], preferred_element_type=jnp.float32
                ).astype(jnp.bfloat16)
                give[it, swap[role]] = product[:block]
                keep[it, role] = product[block:]

        if extra:

            @pl.when((it < items) & (it % quads == 0))
            def _():
                for e in range(extra):

                    @pl.when(r == 0)
                    def _():
                        gate_copy(chunks - extra + e).wait()
                        up_copy(chunks - extra + e).wait()

                    product = jnp.dot(
                        x_buf[r], w_buf[chunks - extra + e], preferred_element_type=jnp.float32
                    ).astype(jnp.bfloat16)
                    give_x[r * extra + e] = product[:block]
                    keep_x[r * extra + e] = product[block:]

        @pl.when((after_core >= 0) & (after_core < items))
        def _():
            first_copy(after_core, other_row(after_core, 1)).start()

        if extra:

            @pl.when((after_core >= 0) & (after_core < items) & (after_core % quads == 0) & (core_row % 2 == 1))
            def _():
                for e in range(extra):
                    first_x_copy(core_row // 2, e).start()

        @pl.when(it < items)
        def _():
            core_copy(it).start()

        if extra:

            @pl.when((it < items) & (it % quads == 0))
            def _():
                for e in range(extra):
                    core_x_copy(r, e).start()

        folding = ((after_first >= quads) & (after_first < 2 * quads)) | (
            (after_first >= 3 * quads) & (after_first < items)
        )

        @pl.when(folding)
        def _():
            for j in (after_first - quads, after_first):
                first_copy(j, j).wait_recv()
                keep[j, 1] = total(keep[j, 1], got_core[j, 1], got_first[j, 1]).astype(jnp.bfloat16)

        if extra:

            @pl.when(after_first == 3 * quads)
            def _():
                for e in range(extra):
                    first_x_copy(1, e).wait_recv()
                    j = 2 * extra + e
                    keep_x[j] = total(keep_x[j], got_core_x[j], got_first_x[extra + e]).astype(jnp.bfloat16)

        @pl.when((it >= magnitude_start) & (it < magnitude_end))
        def _():
            for k in range(2):
                i = 2 * (it - magnitude_start) + k

                @pl.when(i < chunks)
                def _():
                    down_copy(i).wait()
                    sums = lax.dot_general(
                        ones, jnp.abs(d_buf[i]), (((1,), (1,)), ((), ())), preferred_element_type=jnp.float32
                    )[0:1, :]

                    @pl.when(i < items)
                    def _():
                        mag_out[i % ROLES, pl.ds(i // ROLES, 1), :] = sums

                    @pl.when(i >= items)
                    def _():
                        for k in range(ROLES):
                            mag_out[k, pl.ds(quads + i - items, 1), :] = sums

        @pl.when(it == magnitude_end)
        def _():
            for n in range(n_dp - 1):
                magnitude_copy(n).start()
            magnitude[me] = mag_out[chip]

        @pl.when(folding)
        def _():
            for j in (after_first - quads, after_first):
                second_copy(j, other_row(j, 2)).start()

        if extra:

            @pl.when(after_first == 3 * quads)
            def _():
                for e in range(extra):
                    second_x_copy(e).start()

            @pl.when(final == 0)
            def _():
                for e in range(extra):
                    first_x_copy(0, e).wait_recv()
                    second_x_copy(e).wait_recv()
                    shared[me, e : e + 1, :] = squares(
                        total(keep_x[e], got_core_x[e], got_first_x[e], got_second_x[e])
                    )

        @pl.when(final >= 0)
        def _():
            value = jnp.zeros((1, LANES), jnp.float32)
            for k in range(4):
                j = k * quads + final
                second_copy(j, j).wait_recv()
                value = value + squares(total(keep[j, 0], got_core[j, 0], got_first[j, 0], got_second[j]))
            energy[c, pl.ds(final, 1), :] = value

        if extra:

            @pl.when(final == 0)
            def _():
                for n in range(n_dp - 1):
                    share_copy(n).start()

        return on

    lax.fori_loop(0, steps, step, 0)

    energy_copy = remote(energy.at[c], energy.at[c], e_send, e_recv, core_peer)
    energy_copy.start()
    load_groups.wait()
    load_owners.wait()
    for n in range(n_dp - 1):
        magnitude_copy(n).wait_recv()
        if extra:
            share_copy(n).wait_recv()
    mag = magnitude[0]
    for k in range(1, n_dp):
        mag = mag + magnitude[k]
    mag = mag / tok_ref.shape[1]
    if n_tensor > 1:
        pl.semaphore_wait(seen.at[n_tensor - 2], planes)
    tokens = block * n_dp
    if extra:
        both = shared[0]
        for k in range(1, n_dp):
            both = both + shared[k]
        shares = jnp.sqrt(both[:extra] / tokens) * mag[quads : quads + extra]
        shares = jnp.where(chip == 0, shares, 0.0)
    energy_copy.wait()
    score[...] = jnp.sqrt((energy[0] + energy[1]) / tokens) * mag

    lines = lax.broadcasted_iota(jnp.int32, (totals.shape[2], LANES), 0)
    acc = jnp.zeros(lines.shape, jnp.float32)
    for u in range(quads):
        acc = acc + jnp.where(lines == group_buf[pl.ds(ROLES * u + chip, 1), :], score[u : u + 1, :], 0.0)
    for e in range(extra):
        acc = acc + jnp.where(lines == group_buf[items + e : items + e + 1, :], shares[e : e + 1], 0.0)
    slot = ROLES * z + chip
    totals[slot] = jnp.sum(acc.T, axis=0, keepdims=True)
    t_copies = []
    for dz in range(n_tensor):
        for k in range(4):
            if dz or k:
                n = len(t_copies)
                copy = remote(
                    totals.at[slot],
                    totals.at[slot],
                    t_send.at[n],
                    t_recv.at[n],
                    device_at(k % 2, k // 2, True),
                    (z + dz) % n_tensor,
                )
                copy.start()
                t_copies.append(copy)

    for r in range(4):
        for same in (False, True):
            if (r, same) != (0, True):
                token_copy(r, same).wait_send()
    for n in range(n_dp - 1):
        magnitude_copy(n).wait_send()
        if extra:
            share_copy(n).wait_send()

    @pl.loop(0, items)
    def _(j):
        core_copy(j).wait_send()
        first_copy(j, j).wait_send()
        second_copy(j, j).wait_send()

    for e in range(extra):
        for r in range(4):
            core_x_copy(r, e).wait_send()
        for half in range(2):
            first_x_copy(half, e).wait_send()
        second_x_copy(e).wait_send()

    for copy in t_copies:
        copy.wait()
    row = totals[0]
    for k in range(1, ROLES * n_tensor):
        row = row + totals[k]
    row = row[:, : out_ref.shape[1]] / GROUP
    out_ref[...] = jnp.where(owner_buf[...] == z, row, 0.0)


def fused_shards(n_dp, n_tensor, tokens, gate_weight, up_weight, down_weight, channel_group, owners):
    block = tokens.shape[0]
    depth, width = gate_weight.shape
    chunks = width // LANES
    quads, extra = chunks // ROLES, chunks % ROLES
    items, spare = 4 * quads, max(extra, 1)
    count = owners.shape[0]
    span = down_weight.shape[1]
    lines = -(-(quads + extra) // 8) * 8
    padded = -(-count // LANES) * LANES
    peers = n_dp - 1
    far = max(4 * n_tensor - 1, 1)
    vmem = pl.BlockSpec(memory_space=pltpu.VMEM)
    hbm = pl.BlockSpec(memory_space=pl.ANY)
    dma = pltpu.SemaphoreType.DMA
    tile = (block, 2 * LANES)
    half = jnp.bfloat16
    return pl.pallas_call(
        functools.partial(kernel, n_tensor),
        out_shape=jax.ShapeDtypeStruct((1, count), jnp.float32),
        in_specs=[hbm, hbm, hbm, hbm, hbm, hbm],
        out_specs=vmem,
        scratch_shapes=[
            pltpu.VMEM(tokens.shape, half),
            pltpu.VMEM((4, 2 * block, depth), half),
            pltpu.VMEM((chunks, depth, 2 * LANES), half),
            pltpu.VMEM((chunks, LANES, span), half),
            pltpu.VMEM((chunks, LANES), jnp.int32),
            pltpu.VMEM((1, count), jnp.int32),
            pltpu.VMEM((items, ROLES) + tile, half),
            pltpu.VMEM((items, ROLES) + tile, half),
            pltpu.VMEM((items, ROLES) + tile, half),
            pltpu.VMEM((items, 2) + tile, half),
            pltpu.VMEM((items,) + tile, half),
            pltpu.VMEM((4 * spare,) + tile, half),
            pltpu.VMEM((4 * spare,) + tile, half),
            pltpu.VMEM((4 * spare,) + tile, half),
            pltpu.VMEM((2 * spare,) + tile, half),
            pltpu.VMEM((spare,) + tile, half),
            pltpu.VMEM((2, lines, LANES), jnp.float32),
            pltpu.VMEM((n_dp, 8, LANES), jnp.float32),
            pltpu.VMEM((ROLES, lines, LANES), jnp.float32),
            pltpu.VMEM((n_dp, lines, LANES), jnp.float32),
            pltpu.VMEM((lines, LANES), jnp.float32),
            pltpu.VMEM((ROLES * n_tensor, 1, padded), jnp.float32),
            dma((3,)),
            dma((chunks,)),
            dma((chunks,)),
            dma((chunks,)),
            dma((n_dp,)),
            dma((n_dp,)),
            dma((items,)),
            dma((items,)),
            dma((items,)),
            dma((items,)),
            dma((items,)),
            dma((items,)),
            dma((4 * spare,)),
            dma((4 * spare,)),
            dma((2 * spare,)),
            dma((2 * spare,)),
            dma((spare,)),
            dma((spare,)),
            dma((peers,)),
            dma((peers,)),
            dma((peers,)),
            dma((peers,)),
            dma,
            dma,
            dma((far,)),
            dma((far,)),
            pltpu.SemaphoreType.REGULAR((max(n_tensor - 1, 1),)),
        ],
        compiler_params=pltpu.CompilerParams(
            collective_id=0, has_side_effects=True, vmem_limit_bytes=56 * 1024 * 1024
        ),
    )(tokens, gate_weight, up_weight, down_weight, channel_group.reshape(chunks, LANES), owners.reshape(1, count))


def solution(mesh):
    n_dp, n_tensor = mesh.shape["dp"], mesh.shape["tensor"]

    def shards(tokens, gate_weight, *rest):
        if n_dp == 8 and gate_weight.shape[1] % LANES == 0 and gate_weight.shape[1] >= ROLES * LANES:
            return fused_shards(n_dp, n_tensor, tokens, gate_weight, *rest)
        return plain_shards(tokens, gate_weight, *rest)

    return jax.shard_map(
        shards,
        mesh=mesh,
        in_specs=(
            P("dp", None),
            P("dp", "tensor"),
            P("dp", "tensor"),
            P("tensor", "dp"),
            P("tensor"),
            P(),
        ),
        out_specs=P("tensor", None),
        check_vma=False,
    )
```

time: 69.4 us -> 62.2 us (0.90)
  Pallas kernels: 68 us -> 60.8 us
    pallas_call x1, Pallas kernels: 68 us -> 60.8 us  [fused_shards(): pl.pallas_call(functools.partial(kernel, n_tensor), out_shape=jax.ShapeDt...]
where the time goes in v1:
time: 62.2 us; the launch traced here: 62 us
  Pallas kernels  60.8 us (98%)
  local copies, waits for them, and re-layouts  1.19 us (2%)
    pallas_call x1, Pallas kernels, fused_shards(): pl.pallas_call(functools.partial(kernel, n_tensor), out_shape=jax.ShapeDt...  60.8 us

profile of v1, /device:TPU:0, one launch (start us, length us, event | category | flops | bytes accessed | tf_op | source)
XLA Modules:
  0.0 62.0 jit_solution(10902359965749343862)
XLA Ops:
  0.0 60.8 %shard_map.64 = f32[1,116]{1,0:T(1,128)} custom-call(bf16[64,8192]{1,0:T(8,128)(2,1)} %tok_ref.1, bf16[1024,3712]{1,0:T(8,128)(2,1)} %gate_ref.1, bf16[1024,3712]{1,0:T(8,128)(2,1)} %up_ref.1, bf16[3712,1024]{1,0:T(8,128)(2,1)} %down_ref.1, s32[29,128]{1,0:T(8,128)} %bitcast.2, s32[1,116]{1,0:T(1,128)} %bitcast.3), custom_call_target="tpu_custom_call" | custom-call | tf_op jit(solution)/shard_map/pallas_call | solution.py:548
  60.9 1.2 %copy.8 = f32[1,116]{1,0:T(1,128)} copy(f32[1,116]{1,0:T(1,128)} %shard_map.64) | data formatting | bytes 928

commit v2 on v1

--- a/solution.py
+++ b/solution.py
@@ -12,7 +12,13 @@
 ROLES = 4
 LAG_CORE = 2
 LAG_FIRST = 7
+HOLD = 0
 LAG_SECOND = 3
+MAGNITUDES = 3
+MAGNITUDE_ROW = 2
+SPLIT = (2, 3)
+SHARE_SECOND = 4
+SHARE_LAST = 5
 MESH = pl.DeviceIdType.MESH
 
 
@@ -106,7 +112,10 @@
     e_recv,
     t_send,
     t_recv,
+    z_send,
+    z_recv,
     seen,
+    met,
 ):
     n_dp = 8
     chunks = w_buf.shape[0]
@@ -179,18 +188,42 @@
         gate_copy(i).start()
         up_copy(i).start()
 
+    piece = block // n_tensor
+
+    def split(r):
+        return r in SPLIT and n_tensor > 1 and block % (16 * n_tensor) == 0
+
     def token_copy(r, same):
         peer = device_at(r % 2, r // 2, same)
         cols = pl.ds(pl.multiple_of(peer * depth, depth), depth)
         slot = 2 * r + (1 if same else 0)
-        rows = pl.ds(block if same else 0, block)
-        return remote(tok_buf.at[:, cols], x_buf.at[r, rows, :], x_send.at[slot], x_recv.at[slot], peer)
+        start = block if same else 0
+        if split(r):
+            source = pl.ds(pl.multiple_of(z * piece, piece), piece)
+            rows = pl.ds(pl.multiple_of(start + z * piece, piece), piece)
+        else:
+            source, rows = pl.ds(0, block), pl.ds(start, block)
+        return remote(tok_buf.at[source, cols], x_buf.at[r, rows, :], x_send.at[slot], x_recv.at[slot], peer)
+
+    def plane_copies(r):
+        copies = []
+        for same in (False, True):
+            rows = pl.ds(pl.multiple_of((block if same else 0) + z * piece, piece), piece)
+            for dz in range(1, n_tensor):
+                n = (2 * r + (1 if same else 0)) * n_tensor + dz
+                data = x_buf.at[r, rows, :]
+                copies.append(remote(data, data, z_send.at[n], z_recv.at[n], me, (z + dz) % n_tensor))
+        return copies
 
     load_tokens.wait()
     pl.semaphore_wait(barrier, len(near) + planes)
     token_copy(0, False).start()
     for same in (True, False):
         token_copy(1, same).start()
+    for same in (True, False):
+        token_copy(2, same).start()
+    if n_tensor > 2:
+        signal_planes(met.at[0])
     load_groups.start()
     load_owners.start()
 
@@ -250,9 +283,13 @@
         hidden = gate / (1.0 + jnp.exp(-gate)) * up
         return jnp.sum(hidden * hidden, axis=0, keepdims=True)
 
+    def fold(j):
+        first_copy(j, j).wait_recv()
+        keep[j, 1] = total(keep[j, 1], got_core[j, 1], got_first[j, 1]).astype(jnp.bfloat16)
+
     swap = (0, 2, 1, 3)
-    magnitude_start = quads + 1
-    magnitude_end = magnitude_start + -(-chunks // 2)
+    magnitude_start = MAGNITUDE_ROW * quads
+    magnitude_end = magnitude_start + -(-chunks // MAGNITUDES)
     last_fold = 3 * quads + LAG_FIRST
     steps = last_fold + LAG_SECOND + quads
     rounds = [(quads + 2) + 4 * n for n in range(n_tensor - 1)]
@@ -265,22 +302,37 @@
         final = it - last_fold - LAG_SECOND
         r = it // quads
         core_row = after_core // quads
-        for k in range(1, 4):
-
-            @pl.when(it == k * quads)
-            def _():
-                token_copy(k, False).wait_recv()
-                token_copy(k, True).wait_recv()
-
-        @pl.when(it == 2)
+        @pl.when(it == quads)
         def _():
             for same in (True, False):
-                token_copy(2, same).start()
-
-        @pl.when(it == quads)
-        def _():
+                token_copy(1, same).wait_recv()
             for same in (True, False):
                 token_copy(3, same).start()
+
+        for n in range(n_tensor - 2):
+
+            @pl.when(it == 1 + n)
+            def _():
+                pl.semaphore_wait(met.at[n], planes)
+                if n < n_tensor - 3:
+                    signal_planes(met.at[n + 1])
+
+        for k, at in ((2, min(SHARE_SECOND, 2 * quads)), (3, min(quads + SHARE_LAST, 3 * quads))):
+            if split(k):
+
+                @pl.when(it == at)
+                def _():
+                    for same in (True, False):
+                        token_copy(k, same).wait_recv()
+                    for copy in plane_copies(k):
+                        copy.start()
+
+        for k in (2, 3):
+
+            @pl.when(it == k * quads)
+            def _():
+                for copy in plane_copies(k) if split(k) else [token_copy(k, same) for same in (True, False)]:
+                    copy.wait_recv()
 
         for n, at in enumerate(rounds):
 
@@ -362,15 +414,15 @@
                 for e in range(extra):
                     core_x_copy(r, e).start()
 
-        folding = ((after_first >= quads) & (after_first < 2 * quads)) | (
-            (after_first >= 3 * quads) & (after_first < items)
-        )
-
-        @pl.when(folding)
-        def _():
-            for j in (after_first - quads, after_first):
-                first_copy(j, j).wait_recv()
-                keep[j, 1] = total(keep[j, 1], got_core[j, 1], got_first[j, 1]).astype(jnp.bfloat16)
+        early = after_first - HOLD
+        folding = ((after_first >= 3 * quads) & (after_first < items), (early >= quads) & (early < 2 * quads))
+
+        for on_fold, at in zip(folding, (after_first, early)):
+
+            @pl.when(on_fold)
+            def _():
+                for j in (at - quads, at):
+                    fold(j)
 
         if extra:
 
@@ -383,8 +435,8 @@
 
         @pl.when((it >= magnitude_start) & (it < magnitude_end))
         def _():
-            for k in range(2):
-                i = 2 * (it - magnitude_start) + k
+            for k in range(MAGNITUDES):
+                i = MAGNITUDES * (it - magnitude_start) + k
 
                 @pl.when(i < chunks)
                 def _():
@@ -408,10 +460,12 @@
                 magnitude_copy(n).start()
             magnitude[me] = mag_out[chip]
 
-        @pl.when(folding)
-        def _():
-            for j in (after_first - quads, after_first):
-                second_copy(j, other_row(j, 2)).start()
+        for on_fold, at in zip(folding, (after_first, early)):
+
+            @pl.when(on_fold)
+            def _():
+                for j in (at - quads, at):
+                    second_copy(j, other_row(j, 2)).start()
 
         if extra:
 
@@ -501,6 +555,9 @@
         for same in (False, True):
             if (r, same) != (0, True):
                 token_copy(r, same).wait_send()
+        if split(r):
+            for copy in plane_copies(r):
+                copy.wait_send()
     for n in range(n_dp - 1):
         magnitude_copy(n).wait_send()
         if extra:
@@ -599,7 +656,10 @@
             dma,
             dma((far,)),
             dma((far,)),
+            dma((n_dp * n_tensor,)),
+            dma((n_dp * n_tensor,)),
             pltpu.SemaphoreType.REGULAR((max(n_tensor - 1, 1),)),
+            pltpu.SemaphoreType.REGULAR((max(n_tensor - 2, 1),)),
         ],
         compiler_params=pltpu.CompilerParams(
             collective_id=0, has_side_effects=True, vmem_limit_bytes=56 * 1024 * 1024

time: 62.2 us -> 57.9 us (0.931)
  Pallas kernels: 60.8 us -> 56.6 us
    pallas_call x1, Pallas kernels: 60.8 us -> 56.6 us  [fused_shards(): pl.pallas_call(functools.partial(kernel, n_tensor), out_shape=jax.ShapeDt...]
where the time goes in v2:
time: 57.9 us; the launch traced here: 57.8 us
  Pallas kernels  56.6 us (98%)
  local copies, waits for them, and re-layouts  1.19 us (2%)
    pallas_call x1, Pallas kernels, fused_shards(): pl.pallas_call(functools.partial(kernel, n_tensor), out_shape=jax.ShapeDt...  56.6 us
    unnamed x1, local copies, waits for them, and re-layouts  1.19 us

profile of v2, /device:TPU:0, one launch (start us, length us, event | category | flops | bytes accessed | tf_op | source)
XLA Modules:
  0.0 57.8 jit_solution(14008888160092455033)
XLA Ops:
  0.0 56.6 %shard_map.64 = f32[1,116]{1,0:T(1,128)} custom-call(bf16[64,8192]{1,0:T(8,128)(2,1)} %tok_ref.1, bf16[1024,3712]{1,0:T(8,128)(2,1)} %gate_ref.1, bf16[1024,3712]{1,0:T(8,128)(2,1)} %up_ref.1, bf16[3712,1024]{1,0:T(8,128)(2,1)} %down_ref.1, s32[29,128]{1,0:T(8,128)} %bitcast.2, s32[1,116]{1,0:T(1,128)} %bitcast.3), custom_call_target="tpu_custom_call" | custom-call | tf_op jit(solution)/shard_map/pallas_call | solution.py:605
  56.6 1.2 %copy.8 = f32[1,116]{1,0:T(1,128)} copy(f32[1,116]{1,0:T(1,128)} %shard_map.64) | data formatting | bytes 928

commit v3 on v2

--- a/solution.py
+++ b/solution.py
@@ -14,7 +14,6 @@
 LAG_FIRST = 7
 HOLD = 0
 LAG_SECOND = 3
-MAGNITUDES = 3
 MAGNITUDE_ROW = 2
 SPLIT = (2, 3)
 SHARE_SECOND = 4
@@ -87,6 +86,7 @@
     score,
     totals,
     local_sem,
+    tok_sem,
     g_sem,
     u_sem,
     d_sem,
@@ -162,10 +162,32 @@
     planes = jnp.where(z > 0, 1, 0) + jnp.where(z < n_tensor - 1, 1, 0)
     signal_planes(barrier)
 
-    load_tokens = pltpu.make_async_copy(tok_ref, tok_buf, local_sem.at[0])
-    load_groups = pltpu.make_async_copy(group_ref, group_buf, local_sem.at[1])
-    load_owners = pltpu.make_async_copy(owner_ref, owner_buf, local_sem.at[2])
-    load_tokens.start()
+    load_groups = pltpu.make_async_copy(group_ref, group_buf, local_sem.at[0])
+    load_owners = pltpu.make_async_copy(owner_ref, owner_buf, local_sem.at[1])
+    piece = block // n_tensor
+
+    def split(r):
+        return r in SPLIT and n_tensor > 1 and block % (16 * n_tensor) == 0
+
+    def token_rows(r, start):
+        if split(r):
+            return pl.ds(pl.multiple_of(start + z * piece, piece), piece)
+        return pl.ds(start, block)
+
+    def token_columns(f, s, same):
+        return pl.ds(pl.multiple_of(device_at(f, s, same) * depth, depth), depth)
+
+    def token_load(n):
+        f, s, same = others[n]
+        data = (token_rows(f + 2 * s, 0), token_columns(f, s, same))
+        return pltpu.make_async_copy(tok_ref.at[data], tok_buf.at[data], tok_sem.at[n])
+
+    load_own = pltpu.make_async_copy(
+        tok_ref.at[:, token_columns(0, 0, True)], x_buf.at[0, pl.ds(block, block), :], local_sem.at[2]
+    )
+    load_own.start()
+    for n in range(3):
+        token_load(n).start()
 
     def gate_copy(i):
         cols = pl.ds(pl.multiple_of(i * LANES, LANES), LANES)
@@ -179,49 +201,45 @@
         rows = pl.ds(pl.multiple_of(i * LANES, LANES), LANES)
         return pltpu.make_async_copy(down_ref.at[rows, :], d_buf.at[i], d_sem.at[i])
 
-    for i in list(range(ROLES)) + list(range(chunks - extra, chunks)):
+    for i in range(ROLES):
         gate_copy(i).start()
         up_copy(i).start()
-
-    @pl.loop(ROLES, chunks - extra)
+    for n in range(3, len(others)):
+        token_load(n).start()
+
+    @pl.loop(ROLES, chunks)
     def _(i):
         gate_copy(i).start()
         up_copy(i).start()
 
-    piece = block // n_tensor
-
-    def split(r):
-        return r in SPLIT and n_tensor > 1 and block % (16 * n_tensor) == 0
-
     def token_copy(r, same):
-        peer = device_at(r % 2, r // 2, same)
-        cols = pl.ds(pl.multiple_of(peer * depth, depth), depth)
+        cols = token_columns(r % 2, r // 2, same)
         slot = 2 * r + (1 if same else 0)
         start = block if same else 0
-        if split(r):
-            source = pl.ds(pl.multiple_of(z * piece, piece), piece)
-            rows = pl.ds(pl.multiple_of(start + z * piece, piece), piece)
-        else:
-            source, rows = pl.ds(0, block), pl.ds(start, block)
-        return remote(tok_buf.at[source, cols], x_buf.at[r, rows, :], x_send.at[slot], x_recv.at[slot], peer)
+        return remote(
+            tok_buf.at[token_rows(r, 0), cols],
+            x_buf.at[r, token_rows(r, start), :],
+            x_send.at[slot],
+            x_recv.at[slot],
+            device_at(r % 2, r // 2, same),
+        )
 
     def plane_copies(r):
         copies = []
         for same in (False, True):
-            rows = pl.ds(pl.multiple_of((block if same else 0) + z * piece, piece), piece)
+            data = x_buf.at[r, token_rows(r, block if same else 0), :]
             for dz in range(1, n_tensor):
                 n = (2 * r + (1 if same else 0)) * n_tensor + dz
-                data = x_buf.at[r, rows, :]
                 copies.append(remote(data, data, z_send.at[n], z_recv.at[n], me, (z + dz) % n_tensor))
         return copies
 
-    load_tokens.wait()
+    sends = [(f + 2 * s, same) for f, s, same in others]
+    token_load(0).wait()
     pl.semaphore_wait(barrier, len(near) + planes)
-    token_copy(0, False).start()
-    for same in (True, False):
-        token_copy(1, same).start()
-    for same in (True, False):
-        token_copy(2, same).start()
+    token_copy(*sends[0]).start()
+    for n in range(1, 5):
+        token_load(n).wait()
+        token_copy(*sends[n]).start()
     if n_tensor > 2:
         signal_planes(met.at[0])
     load_groups.start()
@@ -231,16 +249,10 @@
     def _(i):
         down_copy(i).start()
 
-    own_cols = pl.ds(pl.multiple_of(me * depth, depth), depth)
-    x_buf[0, block:, :] = tok_buf[:, own_cols]
     mag_out[...] = jnp.zeros_like(mag_out)
     energy[...] = jnp.zeros_like(energy)
     shared[...] = jnp.zeros_like(shared)
     ones = jnp.ones((8, d_buf.shape[2]), jnp.bfloat16)
-
-    def other_row(j, step):
-        r = j // quads
-        return j + quads * (step - 2 * step * ((r // step) % 2))
 
     def core_copy(j):
         return remote(give.at[j], got_core.at[j], core_send.at[j], core_recv.at[j], core_peer)
@@ -283,225 +295,204 @@
         hidden = gate / (1.0 + jnp.exp(-gate)) * up
         return jnp.sum(hidden * hidden, axis=0, keepdims=True)
 
+    swap = (0, 2, 1, 3)
+    role_chips = [chip_at(role // 2, role % 2) for role in range(ROLES)]
+
+    def multiply(r, u, j):
+        for role in (2, 3, 1, 0):
+            product = jnp.dot(
+                x_buf[r], w_buf[ROLES * u + role_chips[role]], preferred_element_type=jnp.float32
+            ).astype(jnp.bfloat16)
+            give[j, swap[role]] = product[:block]
+            keep[j, role] = product[block:]
+
     def fold(j):
         first_copy(j, j).wait_recv()
         keep[j, 1] = total(keep[j, 1], got_core[j, 1], got_first[j, 1]).astype(jnp.bfloat16)
 
-    swap = (0, 2, 1, 3)
+    def finish(j):
+        second_copy(j, j).wait_recv()
+        return squares(total(keep[j, 0], got_core[j, 0], got_first[j, 0], got_second[j]))
+
+    fold_starts = (quads + LAG_FIRST + HOLD, 3 * quads + LAG_FIRST)
+    final_start = fold_starts[1] + LAG_SECOND
+    steps = final_start + quads
     magnitude_start = MAGNITUDE_ROW * quads
-    magnitude_end = magnitude_start + -(-chunks // MAGNITUDES)
-    last_fold = 3 * quads + LAG_FIRST
-    steps = last_fold + LAG_SECOND + quads
-    rounds = [(quads + 2) + 4 * n for n in range(n_tensor - 1)]
-
-    token_copy(0, False).wait_recv()
-
-    def step(it, on):
+
+    def row_at(it, lag):
+        return (it - lag) // quads if 0 <= it - lag < items else None
+
+    def stages(it):
+        return (
+            row_at(it, 0),
+            row_at(it, LAG_CORE),
+            tuple(0 <= it - start < quads for start in fold_starts),
+            0 <= it - magnitude_start < quads,
+            0 <= it - final_start < quads,
+        )
+
+    def step(now, it):
+        row, core_row, folding, weighing, ending = now
         after_core = it - LAG_CORE
-        after_first = it - LAG_FIRST
-        final = it - last_fold - LAG_SECOND
-        r = it // quads
-        core_row = after_core // quads
-        @pl.when(it == quads)
-        def _():
-            for same in (True, False):
-                token_copy(1, same).wait_recv()
-            for same in (True, False):
-                token_copy(3, same).start()
-
-        for n in range(n_tensor - 2):
-
-            @pl.when(it == 1 + n)
-            def _():
-                pl.semaphore_wait(met.at[n], planes)
-                if n < n_tensor - 3:
-                    signal_planes(met.at[n + 1])
-
-        for k, at in ((2, min(SHARE_SECOND, 2 * quads)), (3, min(quads + SHARE_LAST, 3 * quads))):
-            if split(k):
-
-                @pl.when(it == at)
-                def _():
-                    for same in (True, False):
-                        token_copy(k, same).wait_recv()
-                    for copy in plane_copies(k):
-                        copy.start()
-
-        for k in (2, 3):
-
-            @pl.when(it == k * quads)
-            def _():
-                for copy in plane_copies(k) if split(k) else [token_copy(k, same) for same in (True, False)]:
-                    copy.wait_recv()
-
-        for n, at in enumerate(rounds):
-
-            @pl.when(it == at)
-            def _():
-                if n > 0:
-                    pl.semaphore_wait(seen.at[n - 1], planes)
-                signal_planes(seen.at[n])
-
-        @pl.when((after_core >= 0) & (after_core < items))
-        def _():
+        if core_row is not None:
             core_copy(after_core).wait_recv()
             keep[after_core, 2:] = total(keep[after_core, 2:], got_core[after_core, 2:]).astype(jnp.bfloat16)
-
-        if extra:
-
-            @pl.when((after_core >= 0) & (after_core < items) & (after_core % quads == 0))
-            def _():
-                for e in range(extra):
-                    core_x_copy(core_row, e).wait_recv()
-                    j = core_row * extra + e
-                    keep_x[j] = jnp.where(
-                        core_row % 2 == 1, total(keep_x[j], got_core_x[j]), keep_x[j].astype(jnp.float32)
-                    ).astype(jnp.bfloat16)
-
-        @pl.when(it < items)
-        def _():
-            u = it % quads
-
-            @pl.when(r == 0)
-            def _():
+        if row is not None:
+            u = it - row * quads
+            if row == 0:
                 for k in range(ROLES):
                     gate_copy(ROLES * u + k).wait()
                     up_copy(ROLES * u + k).wait()
-
-            for role in (2, 3, 1, 0):
-                product = jnp.dot(
-                    x_buf[r], w_buf[ROLES * u + chip_at(role // 2, role % 2)], preferred_element_type=jnp.float32
-                ).astype(jnp.bfloat16)
-                give[it, swap[role]] = product[:block]
-                keep[it, role] = product[block:]
-
-        if extra:
-
-            @pl.when((it < items) & (it % quads == 0))
-            def _():
-                for e in range(extra):
-
-                    @pl.when(r == 0)
-                    def _():
-                        gate_copy(chunks - extra + e).wait()
-                        up_copy(chunks - extra + e).wait()
-
-                    product = jnp.dot(
-                        x_buf[r], w_buf[chunks - extra + e], preferred_element_type=jnp.float32
-                    ).astype(jnp.bfloat16)
-                    give_x[r * extra + e] = product[:block]
-                    keep_x[r * extra + e] = product[block:]
-
-        @pl.when((after_core >= 0) & (after_core < items))
-        def _():
-            first_copy(after_core, other_row(after_core, 1)).start()
-
-        if extra:
-
-            @pl.when((after_core >= 0) & (after_core < items) & (after_core % quads == 0) & (core_row % 2 == 1))
-            def _():
-                for e in range(extra):
-                    first_x_copy(core_row // 2, e).start()
-
-        @pl.when(it < items)
-        def _():
+            multiply(row, u, it)
+        if core_row is not None:
+            first_copy(after_core, after_core + (-quads if core_row % 2 else quads)).start()
+        if row is not None:
             core_copy(it).start()
-
-        if extra:
-
-            @pl.when((it < items) & (it % quads == 0))
-            def _():
-                for e in range(extra):
-                    core_x_copy(r, e).start()
-
-        early = after_first - HOLD
-        folding = ((after_first >= 3 * quads) & (after_first < items), (early >= quads) & (early < 2 * quads))
-
-        for on_fold, at in zip(folding, (after_first, early)):
-
-            @pl.when(on_fold)
-            def _():
-                for j in (at - quads, at):
-                    fold(j)
-
-        if extra:
-
-            @pl.when(after_first == 3 * quads)
-            def _():
-                for e in range(extra):
-                    first_x_copy(1, e).wait_recv()
-                    j = 2 * extra + e
-                    keep_x[j] = total(keep_x[j], got_core_x[j], got_first_x[extra + e]).astype(jnp.bfloat16)
-
-        @pl.when((it >= magnitude_start) & (it < magnitude_end))
-        def _():
-            for k in range(MAGNITUDES):
-                i = MAGNITUDES * (it - magnitude_start) + k
-
-                @pl.when(i < chunks)
-                def _():
-                    down_copy(i).wait()
-                    sums = lax.dot_general(
-                        ones, jnp.abs(d_buf[i]), (((1,), (1,)), ((), ())), preferred_element_type=jnp.float32
-                    )[0:1, :]
-
-                    @pl.when(i < items)
-                    def _():
-                        mag_out[i % ROLES, pl.ds(i // ROLES, 1), :] = sums
-
-                    @pl.when(i >= items)
-                    def _():
-                        for k in range(ROLES):
-                            mag_out[k, pl.ds(quads + i - items, 1), :] = sums
-
-        @pl.when(it == magnitude_end)
+        for half in range(2):
+            if folding[half]:
+                for r in (2 * half, 2 * half + 1):
+                    fold(it - fold_starts[half] + r * quads)
+        if weighing:
+            v = it - magnitude_start
+            for k in range(ROLES):
+                down_copy(ROLES * v + k).wait()
+            rows = jnp.abs(d_buf[pl.ds(ROLES * v, ROLES)].reshape(ROLES * LANES, d_buf.shape[2]))
+            sums = lax.dot_general(ones, rows, (((1,), (1,)), ((), ())), preferred_element_type=jnp.float32)
+            for k in range(ROLES):
+                mag_out[k, pl.ds(v, 1), :] = sums[0:1, k * LANES : (k + 1) * LANES]
+        for half in range(2):
+            if folding[half]:
+                for r in (2 * half, 2 * half + 1):
+                    j = it - fold_starts[half] + r * quads
+                    second_copy(j, j + (-2 * quads if half else 2 * quads)).start()
+        if folding[1]:
+            u = it - fold_starts[1]
+            energy[c, pl.ds(u, 1), :] = finish(u + 2 * quads) + finish(u + 3 * quads)
+        if ending:
+            u = it - final_start
+            energy[c, pl.ds(u, 1), :] = energy[c, pl.ds(u, 1), :] + (finish(u) + finish(u + quads))
+
+    events = {}
+
+    def at(it):
+        return lambda run: events.setdefault(it, []).append(run)
+
+    @at(quads)
+    def _():
+        for same in (True, False):
+            token_copy(1, same).wait_recv()
+        for n in range(5, 7):
+            token_load(n).wait()
+            token_copy(*sends[n]).start()
+
+    for n in range(n_tensor - 2):
+
+        @at(1 + n)
+        def _(n=n):
+            pl.semaphore_wait(met.at[n], planes)
+            if n < n_tensor - 3:
+                signal_planes(met.at[n + 1])
+
+    for k, when in ((2, min(SHARE_SECOND, 2 * quads)), (3, min(quads + SHARE_LAST, 3 * quads))):
+        if split(k):
+
+            @at(when)
+            def _(k=k):
+                for same in (True, False):
+                    token_copy(k, same).wait_recv()
+                for copy in plane_copies(k):
+                    copy.start()
+
+    for k in (2, 3):
+
+        @at(k * quads)
+        def _(k=k):
+            for copy in plane_copies(k) if split(k) else [token_copy(k, same) for same in (True, False)]:
+                copy.wait_recv()
+
+    for n in range(n_tensor - 1):
+
+        @at(quads + 2 + 4 * n)
+        def _(n=n):
+            if n > 0:
+                pl.semaphore_wait(seen.at[n - 1], planes)
+            signal_planes(seen.at[n])
+
+    for e in range(extra):
+        for r in range(4):
+            when = r * quads if r else min(4, quads - 1)
+
+            @at(when)
+            def _(r=r, e=e):
+                if r == 0:
+                    gate_copy(items + e).wait()
+                    up_copy(items + e).wait()
+                product = jnp.dot(x_buf[r], w_buf[items + e], preferred_element_type=jnp.float32).astype(jnp.bfloat16)
+                give_x[r * extra + e] = product[:block]
+                keep_x[r * extra + e] = product[block:]
+                core_x_copy(r, e).start()
+
+            @at(when + LAG_CORE)
+            def _(r=r, e=e):
+                core_x_copy(r, e).wait_recv()
+                j = r * extra + e
+                if r % 2:
+                    keep_x[j] = total(keep_x[j], got_core_x[j]).astype(jnp.bfloat16)
+                    first_x_copy(r // 2, e).start()
+
+        @at(fold_starts[1])
+        def _(e=e):
+            first_x_copy(1, e).wait_recv()
+            j = 2 * extra + e
+            keep_x[j] = total(keep_x[j], got_core_x[j], got_first_x[extra + e]).astype(jnp.bfloat16)
+            second_x_copy(e).start()
+
+        @at(magnitude_start + quads)
+        def _(e=e):
+            down_copy(items + e).wait()
+            sums = lax.dot_general(
+                ones, jnp.abs(d_buf[items + e]), (((1,), (1,)), ((), ())), preferred_element_type=jnp.float32
+            )
+            for k in range(ROLES):
+                mag_out[k, quads + e : quads + e + 1, :] = sums[0:1, :]
+
+        @at(fold_starts[1] + quads - 1)
+        def _(e=e):
+            first_x_copy(0, e).wait_recv()
+            second_x_copy(e).wait_recv()
+            shared[me, e : e + 1, :] = squares(total(keep_x[e], got_core_x[e], got_first_x[e], got_second_x[e]))
+
+    @at(magnitude_start + quads + 1)
+    def _():
+        for n in range(n_dp - 1):
+            magnitude_copy(n).start()
+        magnitude[me] = mag_out[chip]
+
+    if extra:
+
+        @at(fold_starts[1] + quads)
         def _():
             for n in range(n_dp - 1):
-                magnitude_copy(n).start()
-            magnitude[me] = mag_out[chip]
-
-        for on_fold, at in zip(folding, (after_first, early)):
-
-            @pl.when(on_fold)
-            def _():
-                for j in (at - quads, at):
-                    second_copy(j, other_row(j, 2)).start()
-
-        if extra:
-
-            @pl.when(after_first == 3 * quads)
-            def _():
-                for e in range(extra):
-                    second_x_copy(e).start()
-
-            @pl.when(final == 0)
-            def _():
-                for e in range(extra):
-                    first_x_copy(0, e).wait_recv()
-                    second_x_copy(e).wait_recv()
-                    shared[me, e : e + 1, :] = squares(
-                        total(keep_x[e], got_core_x[e], got_first_x[e], got_second_x[e])
-                    )
-
-        @pl.when(final >= 0)
-        def _():
-            value = jnp.zeros((1, LANES), jnp.float32)
-            for k in range(4):
-                j = k * quads + final
-                second_copy(j, j).wait_recv()
-                value = value + squares(total(keep[j, 0], got_core[j, 0], got_first[j, 0], got_second[j]))
-            energy[c, pl.ds(final, 1), :] = value
-
-        if extra:
-
-            @pl.when(final == 0)
-            def _():
-                for n in range(n_dp - 1):
-                    share_copy(n).start()
-
-        return on
-
-    lax.fori_loop(0, steps, step, 0)
+                share_copy(n).start()
+
+    load_own.wait()
+    token_copy(0, False).wait_recv()
+    low = 0
+    while low < steps:
+        for run in events.pop(low, ()):
+            run()
+        now, high = stages(low), low + 1
+        while high < steps and stages(high) == now and high not in events:
+            high += 1
+        if high == low + 1:
+            step(now, low)
+        else:
+
+            @pl.loop(low, high)
+            def _(it, now=now):
+                step(now, it)
+
+        low = high
 
     energy_copy = remote(energy.at[c], energy.at[c], e_send, e_recv, core_peer)
     energy_copy.start()
@@ -631,6 +622,7 @@
             pltpu.VMEM((lines, LANES), jnp.float32),
             pltpu.VMEM((ROLES * n_tensor, 1, padded), jnp.float32),
             dma((3,)),
+            dma((peers,)),
             dma((chunks,)),
             dma((chunks,)),
             dma((chunks,)),

time: 57.9 us -> 56.7 us (0.979)
  Pallas kernels: 56.6 us -> 55.4 us
    pallas_call x1, Pallas kernels: 56.6 us -> 55.4 us  [fused_shards(): pl.pallas_call(functools.partial(kernel, n_tensor), out_shape=jax.ShapeDt...]
where the time goes in v3:
time: 56.7 us; the launch traced here: 56.6 us
  Pallas kernels  55.4 us (98%)
  local copies, waits for them, and re-layouts  1.19 us (2%)
    pallas_call x1, Pallas kernels, fused_shards(): pl.pallas_call(functools.partial(kernel, n_tensor), out_shape=jax.ShapeDt...  55.4 us
    unnamed x1, local copies, waits for them, and re-layouts  1.19 us

profile of v3, /device:TPU:0, one launch (start us, length us, event | category | flops | bytes accessed | tf_op | source)
XLA Modules:
  0.0 56.6 jit_solution(13207755617839926441)
XLA Ops:
  0.0 55.4 %shard_map.64 = f32[1,116]{1,0:T(1,128)} custom-call(bf16[64,8192]{1,0:T(8,128)(2,1)} %tok_ref.1, bf16[1024,3712]{1,0:T(8,128)(2,1)} %gate_ref.1, bf16[1024,3712]{1,0:T(8,128)(2,1)} %up_ref.1, bf16[3712,1024]{1,0:T(8,128)(2,1)} %down_ref.1, s32[29,128]{1,0:T(8,128)} %bitcast.2, s32[1,116]{1,0:T(1,128)} %bitcast.3), custom_call_target="tpu_custom_call" | custom-call | tf_op jit(solution)/shard_map/pallas_call | solution.py:596
  55.4 1.2 %copy.8 = f32[1,116]{1,0:T(1,128)} copy(f32[1,116]{1,0:T(1,128)} %shard_map.64) | data formatting | bytes 928

commit v4 on v3

--- a/solution.py
+++ b/solution.py
@@ -87,9 +87,7 @@
     totals,
     local_sem,
     tok_sem,
-    g_sem,
-    u_sem,
-    d_sem,
+    w_sem,
     x_send,
     x_recv,
     core_send,
@@ -191,15 +189,17 @@
 
     def gate_copy(i):
         cols = pl.ds(pl.multiple_of(i * LANES, LANES), LANES)
-        return pltpu.make_async_copy(gate_ref.at[:, cols], w_buf.at[i, :, pl.ds(0, LANES)], g_sem.at[i])
+        return pltpu.make_async_copy(gate_ref.at[:, cols], w_buf.at[i, :, pl.ds(0, LANES)], w_sem.at[i // ROLES])
 
     def up_copy(i):
         cols = pl.ds(pl.multiple_of(i * LANES, LANES), LANES)
-        return pltpu.make_async_copy(up_ref.at[:, cols], w_buf.at[i, :, pl.ds(LANES, LANES)], u_sem.at[i])
-
-    def down_copy(i):
-        rows = pl.ds(pl.multiple_of(i * LANES, LANES), LANES)
-        return pltpu.make_async_copy(down_ref.at[rows, :], d_buf.at[i], d_sem.at[i])
+        return pltpu.make_async_copy(up_ref.at[:, cols], w_buf.at[i, :, pl.ds(LANES, LANES)], w_sem.at[i // ROLES])
+
+    def wait_weights(u, count):
+        data = w_buf.at[pl.ds(ROLES * u, count)]
+        pltpu.make_async_copy(data, data, w_sem.at[u]).wait()
+
+    load_down = pltpu.make_async_copy(down_ref, d_buf, local_sem.at[3])
 
     for i in range(ROLES):
         gate_copy(i).start()
@@ -229,9 +229,12 @@
         for same in (False, True):
             data = x_buf.at[r, token_rows(r, block if same else 0), :]
             for dz in range(1, n_tensor):
-                n = (2 * r + (1 if same else 0)) * n_tensor + dz
-                copies.append(remote(data, data, z_send.at[n], z_recv.at[n], me, (z + dz) % n_tensor))
+                copies.append(remote(data, data, z_send.at[r], z_recv.at[r], me, (z + dz) % n_tensor))
         return copies
+
+    def plane_rows(r):
+        data = x_buf.at[r, pl.ds(0, 2 * (n_tensor - 1) * piece), :]
+        return remote(data, data, z_send.at[r], z_recv.at[r], me)
 
     sends = [(f + 2 * s, same) for f, s, same in others]
     token_load(0).wait()
@@ -245,23 +248,30 @@
     load_groups.start()
     load_owners.start()
 
-    @pl.loop(0, chunks)
-    def _(i):
-        down_copy(i).start()
-
+    load_down.start()
     mag_out[...] = jnp.zeros_like(mag_out)
     energy[...] = jnp.zeros_like(energy)
     shared[...] = jnp.zeros_like(shared)
-    ones = jnp.ones((8, d_buf.shape[2]), jnp.bfloat16)
+    ones = jnp.ones((8, d_buf.shape[1]), jnp.bfloat16)
 
     def core_copy(j):
-        return remote(give.at[j], got_core.at[j], core_send.at[j], core_recv.at[j], core_peer)
-
-    def first_copy(j, to):
-        return remote(keep.at[j, pl.ds(2, 2)], got_first.at[to], first_send.at[j], first_recv.at[to], first_peer)
-
-    def second_copy(j, to):
-        return remote(keep.at[j, 1], got_second.at[to], second_send.at[j], second_recv.at[to], second_peer)
+        return remote(give.at[j], got_core.at[j], core_send, core_recv.at[j], core_peer)
+
+    def first_copy(r, u):
+        to, sem = got_first.at[r + 1 - 2 * (r % 2), u], first_recv.at[r // 2, u]
+        return remote(keep.at[r * quads + u, pl.ds(2, 2)], to, first_send, sem, first_peer)
+
+    def second_copy(r, u):
+        to, sem = got_second.at[(r + 2) % 4, u], second_recv.at[(r + 2) % 4 // 2, u]
+        return remote(keep.at[r * quads + u, 1], to, second_send, sem, second_peer)
+
+    def wait_first(half, u):
+        data = got_first.at[pl.ds(2 * half, 2), u]
+        remote(data, data, first_send, first_recv.at[half, u], first_peer).wait_recv()
+
+    def wait_second(half, u):
+        data = got_second.at[pl.ds(2 * half, 2), u]
+        remote(data, data, second_send, second_recv.at[half, u], second_peer).wait_recv()
 
     def core_x_copy(r, e):
         j = r * extra + e
@@ -278,11 +288,11 @@
         )
 
     def share_copy(n):
-        return remote(shared.at[me], shared.at[me], s_send.at[n], s_recv.at[n], device_at(*others[n]))
+        return remote(shared.at[me], shared.at[me], s_send, s_recv, device_at(*others[n]))
 
     def magnitude_copy(n):
         f, s, same = others[n]
-        return remote(mag_out.at[chip_at(f, s)], magnitude.at[me], m_send.at[n], m_recv.at[n], device_at(f, s, same))
+        return remote(mag_out.at[chip_at(f, s)], magnitude.at[me], m_send, m_recv, device_at(f, s, same))
 
     def total(*refs):
         value = refs[0].astype(jnp.float32)
@@ -306,13 +316,19 @@
             give[j, swap[role]] = product[:block]
             keep[j, role] = product[block:]
 
-    def fold(j):
-        first_copy(j, j).wait_recv()
-        keep[j, 1] = total(keep[j, 1], got_core[j, 1], got_first[j, 1]).astype(jnp.bfloat16)
-
-    def finish(j):
-        second_copy(j, j).wait_recv()
-        return squares(total(keep[j, 0], got_core[j, 0], got_first[j, 0], got_second[j]))
+    def fold(half, u):
+        wait_first(half, u)
+        for r in (2 * half, 2 * half + 1):
+            j = r * quads + u
+            keep[j, 1] = total(keep[j, 1], got_core[j, 1], got_first[r, u, 1]).astype(jnp.bfloat16)
+
+    def finish(half, u):
+        wait_second(half, u)
+        parts = []
+        for r in (2 * half, 2 * half + 1):
+            j = r * quads + u
+            parts.append(squares(total(keep[j, 0], got_core[j, 0], got_first[r, u, 0], got_second[r, u])))
+        return parts[0] + parts[1]
 
     fold_starts = (quads + LAG_FIRST + HOLD, 3 * quads + LAG_FIRST)
     final_start = fold_starts[1] + LAG_SECOND
@@ -340,37 +356,31 @@
         if row is not None:
             u = it - row * quads
             if row == 0:
-                for k in range(ROLES):
-                    gate_copy(ROLES * u + k).wait()
-                    up_copy(ROLES * u + k).wait()
+                wait_weights(u, ROLES)
             multiply(row, u, it)
         if core_row is not None:
-            first_copy(after_core, after_core + (-quads if core_row % 2 else quads)).start()
+            first_copy(core_row, after_core - core_row * quads).start()
         if row is not None:
             core_copy(it).start()
         for half in range(2):
             if folding[half]:
-                for r in (2 * half, 2 * half + 1):
-                    fold(it - fold_starts[half] + r * quads)
+                fold(half, it - fold_starts[half])
         if weighing:
             v = it - magnitude_start
-            for k in range(ROLES):
-                down_copy(ROLES * v + k).wait()
-            rows = jnp.abs(d_buf[pl.ds(ROLES * v, ROLES)].reshape(ROLES * LANES, d_buf.shape[2]))
+            rows = jnp.abs(d_buf[pl.ds(pl.multiple_of(ROLES * LANES * v, LANES), ROLES * LANES), :])
             sums = lax.dot_general(ones, rows, (((1,), (1,)), ((), ())), preferred_element_type=jnp.float32)
             for k in range(ROLES):
                 mag_out[k, pl.ds(v, 1), :] = sums[0:1, k * LANES : (k + 1) * LANES]
         for half in range(2):
             if folding[half]:
                 for r in (2 * half, 2 * half + 1):
-                    j = it - fold_starts[half] + r * quads
-                    second_copy(j, j + (-2 * quads if half else 2 * quads)).start()
+                    second_copy(r, it - fold_starts[half]).start()
         if folding[1]:
             u = it - fold_starts[1]
-            energy[c, pl.ds(u, 1), :] = finish(u + 2 * quads) + finish(u + 3 * quads)
+            energy[c, pl.ds(u, 1), :] = finish(1, u)
         if ending:
             u = it - final_start
-            energy[c, pl.ds(u, 1), :] = energy[c, pl.ds(u, 1), :] + (finish(u) + finish(u + quads))
+            energy[c, pl.ds(u, 1), :] = energy[c, pl.ds(u, 1), :] + finish(0, u)
 
     events = {}
 
@@ -407,7 +417,7 @@
 
         @at(k * quads)
         def _(k=k):
-            for copy in plane_copies(k) if split(k) else [token_copy(k, same) for same in (True, False)]:
+            for copy in [plane_rows(k)] if split(k) else [token_copy(k, same) for same in (True, False)]:
                 copy.wait_recv()
 
     for n in range(n_tensor - 1):
@@ -420,13 +430,12 @@
 
     for e in range(extra):
         for r in range(4):
-            when = r * quads if r else min(4, quads - 1)
+            when = r * quads if r else quads - 1
 
             @at(when)
             def _(r=r, e=e):
-                if r == 0:
-                    gate_copy(items + e).wait()
-                    up_copy(items + e).wait()
+                if r == 0 and e == 0:
+                    wait_weights(quads, extra)
                 product = jnp.dot(x_buf[r], w_buf[items + e], preferred_element_type=jnp.float32).astype(jnp.bfloat16)
                 give_x[r * extra + e] = product[:block]
                 keep_x[r * extra + e] = product[block:]
@@ -449,10 +458,8 @@
 
         @at(magnitude_start + quads)
         def _(e=e):
-            down_copy(items + e).wait()
-            sums = lax.dot_general(
-                ones, jnp.abs(d_buf[items + e]), (((1,), (1,)), ((), ())), preferred_element_type=jnp.float32
-            )
+            rows = jnp.abs(d_buf[(items + e) * LANES : (items + e + 1) * LANES, :])
+            sums = lax.dot_general(ones, rows, (((1,), (1,)), ((), ())), preferred_element_type=jnp.float32)
             for k in range(ROLES):
                 mag_out[k, quads + e : quads + e + 1, :] = sums[0:1, :]
 
@@ -475,6 +482,7 @@
             for n in range(n_dp - 1):
                 share_copy(n).start()
 
+    at(magnitude_start)(load_down.wait)
     load_own.wait()
     token_copy(0, False).wait_recv()
     low = 0
@@ -498,10 +506,13 @@
     energy_copy.start()
     load_groups.wait()
     load_owners.wait()
-    for n in range(n_dp - 1):
-        magnitude_copy(n).wait_recv()
-        if extra:
-            share_copy(n).wait_recv()
+    all_magnitudes = magnitude.at[pl.ds(0, n_dp - 1)]
+    magnitudes = remote(all_magnitudes, all_magnitudes, m_send, m_recv, core_peer)
+    magnitudes.wait_recv()
+    all_shares = shared.at[pl.ds(0, n_dp - 1)]
+    shares_in = remote(all_shares, all_shares, s_send, s_recv, core_peer)
+    if extra:
+        shares_in.wait_recv()
     mag = magnitude[0]
     for k in range(1, n_dp):
         mag = mag + magnitude[k]
@@ -526,40 +537,31 @@
         acc = acc + jnp.where(lines == group_buf[items + e : items + e + 1, :], shares[e : e + 1], 0.0)
     slot = ROLES * z + chip
     totals[slot] = jnp.sum(acc.T, axis=0, keepdims=True)
-    t_copies = []
     for dz in range(n_tensor):
         for k in range(4):
             if dz or k:
-                n = len(t_copies)
-                copy = remote(
+                remote(
                     totals.at[slot],
                     totals.at[slot],
-                    t_send.at[n],
-                    t_recv.at[n],
+                    t_send,
+                    t_recv,
                     device_at(k % 2, k // 2, True),
                     (z + dz) % n_tensor,
-                )
-                copy.start()
-                t_copies.append(copy)
-
-    for r in range(4):
-        for same in (False, True):
-            if (r, same) != (0, True):
-                token_copy(r, same).wait_send()
-        if split(r):
-            for copy in plane_copies(r):
-                copy.wait_send()
-    for n in range(n_dp - 1):
-        magnitude_copy(n).wait_send()
-        if extra:
-            share_copy(n).wait_send()
-
-    @pl.loop(0, items)
-    def _(j):
-        core_copy(j).wait_send()
-        first_copy(j, j).wait_send()
-        second_copy(j, j).wait_send()
-
+                ).start()
+
+    for send in sends:
+        token_copy(*send).wait_send()
+    for k in SPLIT:
+        if split(k):
+            plane_rows(k).wait_send()
+    magnitudes.wait_send()
+    if extra:
+        shares_in.wait_send()
+    remote(give, give, core_send, core_recv.at[0], core_peer).wait_send()
+    first_part = keep.at[:, pl.ds(2, 2)]
+    remote(first_part, first_part, first_send, core_recv.at[0], core_peer).wait_send()
+    second_part = keep.at[:, 1]
+    remote(second_part, second_part, second_send, core_recv.at[0], core_peer).wait_send()
     for e in range(extra):
         for r in range(4):
             core_x_copy(r, e).wait_send()
@@ -567,8 +569,10 @@
             first_x_copy(half, e).wait_send()
         second_x_copy(e).wait_send()
 
-    for copy in t_copies:
-        copy.wait()
+    far = ROLES * n_tensor - 1
+    all_totals = totals.at[pl.ds(0, far)]
+    arrived = remote(all_totals, all_totals, t_send, t_recv, core_peer)
+    arrived.wait()
     row = totals[0]
     for k in range(1, ROLES * n_tensor):
         row = row + totals[k]
@@ -587,7 +591,6 @@
     lines = -(-(quads + extra) // 8) * 8
     padded = -(-count // LANES) * LANES
     peers = n_dp - 1
-    far = max(4 * n_tensor - 1, 1)
     vmem = pl.BlockSpec(memory_space=pltpu.VMEM)
     hbm = pl.BlockSpec(memory_space=pl.ANY)
     dma = pltpu.SemaphoreType.DMA
@@ -602,14 +605,14 @@
             pltpu.VMEM(tokens.shape, half),
             pltpu.VMEM((4, 2 * block, depth), half),
             pltpu.VMEM((chunks, depth, 2 * LANES), half),
-            pltpu.VMEM((chunks, LANES, span), half),
+            pltpu.VMEM((width, span), half),
             pltpu.VMEM((chunks, LANES), jnp.int32),
             pltpu.VMEM((1, count), jnp.int32),
             pltpu.VMEM((items, ROLES) + tile, half),
             pltpu.VMEM((items, ROLES) + tile, half),
             pltpu.VMEM((items, ROLES) + tile, half),
-            pltpu.VMEM((items, 2) + tile, half),
-            pltpu.VMEM((items,) + tile, half),
+            pltpu.VMEM((4, quads, 2) + tile, half),
+            pltpu.VMEM((4, quads) + tile, half),
             pltpu.VMEM((4 * spare,) + tile, half),
             pltpu.VMEM((4 * spare,) + tile, half),
             pltpu.VMEM((4 * spare,) + tile, half),
@@ -621,35 +624,33 @@
             pltpu.VMEM((n_dp, lines, LANES), jnp.float32),
             pltpu.VMEM((lines, LANES), jnp.float32),
             pltpu.VMEM((ROLES * n_tensor, 1, padded), jnp.float32),
-            dma((3,)),
+            dma((4,)),
             dma((peers,)),
-            dma((chunks,)),
-            dma((chunks,)),
-            dma((chunks,)),
+            dma((quads + 1,)),
             dma((n_dp,)),
             dma((n_dp,)),
+            dma,
             dma((items,)),
-            dma((items,)),
-            dma((items,)),
-            dma((items,)),
-            dma((items,)),
-            dma((items,)),
+            dma,
+            dma((2, quads)),
+            dma,
+            dma((2, quads)),
             dma((4 * spare,)),
             dma((4 * spare,)),
             dma((2 * spare,)),
             dma((2 * spare,)),
             dma((spare,)),
             dma((spare,)),
-            dma((peers,)),
-            dma((peers,)),
-            dma((peers,)),
-            dma((peers,)),
-            dma,
-            dma,
-            dma((far,)),
-            dma((far,)),
-            dma((n_dp * n_tensor,)),
-            dma((n_dp * n_tensor,)),
+            dma,
+            dma,
+            dma,
+            dma,
+            dma,
+            dma,
+            dma,
+            dma,
+            dma((4,)),
+            dma((4,)),
             pltpu.SemaphoreType.REGULAR((max(n_tensor - 1, 1),)),
             pltpu.SemaphoreType.REGULAR((max(n_tensor - 2, 1),)),
         ],

time: 56.7 us -> 53 us (0.935)
  Pallas kernels: 55.4 us -> 51.6 us
    pallas_call x1, Pallas kernels: 55.4 us -> 51.6 us  [fused_shards(): pl.pallas_call(functools.partial(kernel, n_tensor), out_shape=jax.ShapeDt...]
where the time goes in v4:
time: 53 us; the launch traced here: 52.8 us
  Pallas kernels  51.6 us (97%)
  local copies, waits for them, and re-layouts  1.19 us (2%)
    pallas_call x1, Pallas kernels, fused_shards(): pl.pallas_call(functools.partial(kernel, n_tensor), out_shape=jax.ShapeDt...  51.6 us
    unnamed x1, local copies, waits for them, and re-layouts  1.19 us

profile of v4, /device:TPU:0, one launch (start us, length us, event | category | flops | bytes accessed | tf_op | source)
XLA Modules:
  0.0 52.8 jit_solution(1763328248442105659)
XLA Ops:
  0.0 51.6 %shard_map.64 = f32[1,116]{1,0:T(1,128)} custom-call(bf16[64,8192]{1,0:T(8,128)(2,1)} %tok_ref.1, bf16[1024,3712]{1,0:T(8,128)(2,1)} %gate_ref.1, bf16[1024,3712]{1,0:T(8,128)(2,1)} %up_ref.1, bf16[3712,1024]{1,0:T(8,128)(2,1)} %down_ref.1, s32[29,128]{1,0:T(8,128)} %bitcast.2, s32[1,116]{1,0:T(1,128)} %bitcast.3), custom_call_target="tpu_custom_call" | custom-call | tf_op jit(solution)/shard_map/pallas_call | solution.py:599
  51.6 1.2 %copy.8 = f32[1,116]{1,0:T(1,128)} copy(f32[1,116]{1,0:T(1,128)} %shard_map.64) | data formatting | bytes 928

commit v5 on v4

--- a/solution.py
+++ b/solution.py
@@ -214,27 +214,33 @@
 
     def token_copy(r, same):
         cols = token_columns(r % 2, r // 2, same)
-        slot = 2 * r + (1 if same else 0)
         start = block if same else 0
         return remote(
             tok_buf.at[token_rows(r, 0), cols],
             x_buf.at[r, token_rows(r, start), :],
-            x_send.at[slot],
-            x_recv.at[slot],
+            x_send.at[1 if split(r) else 0],
+            x_recv.at[r],
             device_at(r % 2, r // 2, same),
         )
+
+    def wait_tokens(r):
+        if split(r):
+            data = x_buf.at[r, pl.ds(0, 2 * piece), :]
+        else:
+            data = x_buf.at[r, pl.ds(0, 2 * block if r else block), :]
+        remote(data, data, x_send.at[0], x_recv.at[r], core_peer).wait_recv()
 
     def plane_copies(r):
         copies = []
         for same in (False, True):
             data = x_buf.at[r, token_rows(r, block if same else 0), :]
             for dz in range(1, n_tensor):
-                copies.append(remote(data, data, z_send.at[r], z_recv.at[r], me, (z + dz) % n_tensor))
+                copies.append(remote(data, data, z_send.at[r // 3], z_recv.at[r // 3], me, (z + dz) % n_tensor))
         return copies
 
     def plane_rows(r):
         data = x_buf.at[r, pl.ds(0, 2 * (n_tensor - 1) * piece), :]
-        return remote(data, data, z_send.at[r], z_recv.at[r], me)
+        return remote(data, data, z_send.at[r // 3], z_recv.at[r // 3], core_peer)
 
     sends = [(f + 2 * s, same) for f, s, same in others]
     token_load(0).wait()
@@ -275,16 +281,16 @@
 
     def core_x_copy(r, e):
         j = r * extra + e
-        return remote(give_x.at[j], got_core_x.at[j], core_x_send.at[j], core_x_recv.at[j], core_peer)
+        return remote(give_x.at[j], got_core_x.at[j], core_x_send, core_x_recv.at[j], core_peer)
 
     def first_x_copy(half, e):
         j = half * extra + e
         source = (2 * half + 1) * extra + e
-        return remote(keep_x.at[source], got_first_x.at[j], first_x_send.at[j], first_x_recv.at[j], first_peer)
+        return remote(keep_x.at[source], got_first_x.at[j], first_x_send, first_x_recv.at[j], first_peer)
 
     def second_x_copy(e):
         return remote(
-            keep_x.at[2 * extra + e], got_second_x.at[e], second_x_send.at[e], second_x_recv.at[e], second_peer
+            keep_x.at[2 * extra + e], got_second_x.at[e], second_x_send, second_x_recv.at[e], second_peer
         )
 
     def share_copy(n):
@@ -389,8 +395,7 @@
 
     @at(quads)
     def _():
-        for same in (True, False):
-            token_copy(1, same).wait_recv()
+        wait_tokens(1)
         for n in range(5, 7):
             token_load(n).wait()
             token_copy(*sends[n]).start()
@@ -408,8 +413,7 @@
 
             @at(when)
             def _(k=k):
-                for same in (True, False):
-                    token_copy(k, same).wait_recv()
+                wait_tokens(k)
                 for copy in plane_copies(k):
                     copy.start()
 
@@ -417,8 +421,10 @@
 
         @at(k * quads)
         def _(k=k):
-            for copy in [plane_rows(k)] if split(k) else [token_copy(k, same) for same in (True, False)]:
-                copy.wait_recv()
+            if split(k):
+                plane_rows(k).wait_recv()
+            else:
+                wait_tokens(k)
 
     for n in range(n_tensor - 1):
 
@@ -484,7 +490,7 @@
 
     at(magnitude_start)(load_down.wait)
     load_own.wait()
-    token_copy(0, False).wait_recv()
+    wait_tokens(0)
     low = 0
     while low < steps:
         for run in events.pop(low, ()):
@@ -549,8 +555,11 @@
                     (z + dz) % n_tensor,
                 ).start()
 
-    for send in sends:
-        token_copy(*send).wait_send()
+    for cut in (False, True):
+        count = sum(split(r) == cut for r, _ in sends)
+        if count:
+            data = tok_buf.at[pl.ds(0, piece if cut else block), pl.ds(0, count * depth)]
+            remote(data, data, x_send.at[1 if cut else 0], x_recv.at[0], core_peer).wait_send()
     for k in SPLIT:
         if split(k):
             plane_rows(k).wait_send()
@@ -562,12 +571,9 @@
     remote(first_part, first_part, first_send, core_recv.at[0], core_peer).wait_send()
     second_part = keep.at[:, 1]
     remote(second_part, second_part, second_send, core_recv.at[0], core_peer).wait_send()
-    for e in range(extra):
-        for r in range(4):
-            core_x_copy(r, e).wait_send()
-        for half in range(2):
-            first_x_copy(half, e).wait_send()
-        second_x_copy(e).wait_send()
+    if extra:
+        for ref, sem in ((give_x, core_x_send), (got_first_x, first_x_send), (got_second_x, second_x_send)):
+            remote(ref, ref, sem, core_recv.at[0], core_peer).wait_send()
 
     far = ROLES * n_tensor - 1
     all_totals = totals.at[pl.ds(0, far)]
@@ -627,30 +633,30 @@
             dma((4,)),
             dma((peers,)),
             dma((quads + 1,)),
-            dma((n_dp,)),
-            dma((n_dp,)),
+            dma((2,)),
+            dma((4,)),
             dma,
             dma((items,)),
             dma,
             dma((2, quads)),
             dma,
             dma((2, quads)),
+            dma,
             dma((4 * spare,)),
-            dma((4 * spare,)),
+            dma,
             dma((2 * spare,)),
-            dma((2 * spare,)),
+            dma,
             dma((spare,)),
-            dma((spare,)),
-            dma,
-            dma,
-            dma,
-            dma,
-            dma,
-            dma,
-            dma,
-            dma,
-            dma((4,)),
-            dma((4,)),
+            dma,
+            dma,
+            dma,
+            dma,
+            dma,
+            dma,
+            dma,
+            dma,
+            dma((2,)),
+            dma((2,)),
             pltpu.SemaphoreType.REGULAR((max(n_tensor - 1, 1),)),
             pltpu.SemaphoreType.REGULAR((max(n_tensor - 2, 1),)),
         ],

time: 53 us -> 52.8 us (level)
  no operation moved by 1% of the time
where the time goes in v5:
time: 52.8 us; the launch traced here: 52.6 us
  Pallas kernels  51.4 us (97%)
  local copies, waits for them, and re-layouts  1.19 us (2%)
    pallas_call x1, Pallas kernels, fused_shards(): pl.pallas_call(functools.partial(kernel, n_tensor), out_shape=jax.ShapeDt...  51.4 us
    unnamed x1, local copies, waits for them, and re-layouts  1.19 us

profile of v5, /device:TPU:0, one launch (start us, length us, event | category | flops | bytes accessed | tf_op | source)
XLA Modules:
  0.0 52.6 jit_solution(5670618694445349914)
XLA Ops:
  0.0 51.4 %shard_map.64 = f32[1,116]{1,0:T(1,128)} custom-call(bf16[64,8192]{1,0:T(8,128)(2,1)} %tok_ref.1, bf16[1024,3712]{1,0:T(8,128)(2,1)} %gate_ref.1, bf16[1024,3712]{1,0:T(8,128)(2,1)} %up_ref.1, bf16[3712,1024]{1,0:T(8,128)(2,1)} %down_ref.1, s32[29,128]{1,0:T(8,128)} %bitcast.2, s32[1,116]{1,0:T(1,128)} %bitcast.3), custom_call_target="tpu_custom_call" | custom-call | tf_op jit(solution)/shard_map/pallas_call | solution.py:605
  51.5 1.2 %copy.8 = f32[1,116]{1,0:T(1,128)} copy(f32[1,116]{1,0:T(1,128)} %shard_map.64) | data formatting | bytes 928
